TPU v7x, 32 devices: a whole 2x2x4 slice. The times are simulated.
32 devices in a mesh: ctx: 8 (over y, x, core), dp: 4 (over z).
Axes of the slice: x: 2, y: 2, z: 4, core: 2. Of those that a mesh axis runs over, the one named last changes fastest.
Arguments:
- query_previous: bfloat16 [4, 1024, 2048], P('dp', 'ctx'), may hold values from -240 to 240
- key_previous: bfloat16 [4, 1024, 512], P('dp', 'ctx'), may hold values from -6 to 6
- value_previous: bfloat16 [4, 1024, 512], P('dp', 'ctx'), may hold values from -6 to 6
- span_order: int32 [16], replicated, may hold values from 0 to 15, each once
- resid: bfloat16 [4, 1024, 4096], P('dp', 'ctx'), may hold values from -6 to 6
- grad_norm: bfloat16 [4, 1024, 4096], P('dp', 'ctx'), may hold values from -3 to 3
- gain: float32 [4096], replicated, may hold values from 0.1 to 1.9
Outputs:
- out_prev: bfloat16 [4, 1024, 2048], P('dp', 'ctx')
- lse_prev: float32 [4, 16, 1024], P('dp', None, 'ctx')
- resid_grad: bfloat16 [4, 1024, 4096], P('dp', 'ctx')
- gain_grad: float32 [4096], replicated
Inputs may be any that keep to these rules, and one draw needn't show every extreme that they name: span_order names each of the 16 spans once; rows c * 64 to (c + 1) * 64 - 1 of a sequence's arrays hold span span_order[c].
All inputs are finite; a program needn't handle non-finite values.
Results may differ from a plain program's by a relative error of at most 0.0055.
Values may be sent and summed in bfloat16 or wider, within the bound.
A program may use at most 64 MiB of HBM per device.

v0:
```python
import math

import jax
import jax.numpy as jnp
from jax import lax
from jax.sharding import PartitionSpec as P

QUERY_HEADS = 16
KEY_VALUE_HEADS = 4
HEAD_WIDTH = 128


def key_positions(tally_count, span_order, half):
    index = jnp.arange(tally_count, dtype=jnp.int32)
    slot = index // half
    table = slot[:, None] == jnp.arange(span_order.shape[0], dtype=jnp.int32)[None, :]
    chosen = jnp.sum(jnp.where(table, span_order[None, :], 0), axis=1)
    return chosen * half + index % half


def dense_update(query_rows, q_positions, carry, key_rows, value_rows, k_positions):
    top, total, summed = carry
    scores = jnp.einsum(
        "rkgd,skd->kgrs", query_rows, key_rows, preferred_element_type=jnp.float32
    ) * HEAD_WIDTH ** (-0.5)
    mask = (k_positions[None, :] <= q_positions[:, None])[None, None]
    scores = jnp.where(mask, scores, -1e30)
    new_top = jnp.maximum(top, jnp.max(scores, axis=-1))
    weights = jnp.where(mask, jnp.exp(scores - new_top[..., None]), 0.0)
    factor = jnp.exp(top - new_top)
    total = total * factor + jnp.sum(weights, axis=-1)
    probs = weights.astype(jnp.bfloat16)
    added = jnp.einsum("kgrs,skd->rkgd", probs, value_rows, preferred_element_type=jnp.float32)
    summed = summed * jnp.transpose(factor, (2, 0, 1))[..., None] + added
    return (new_top, total, summed)


def update(query_rows, q_positions, carry, key_rows, value_rows, k_positions):
    later = jnp.min(k_positions) > jnp.max(q_positions)
    return lax.cond(
        later,
        lambda state: state,
        lambda state: dense_update(
            query_rows, q_positions, state, key_rows, value_rows, k_positions
        ),
        carry,
    )


def fold_piece(query_rows, q_positions, carry, k_piece, v_piece, span_order, half):
    tally_count = k_piece.shape[1]
    heads = k_piece.shape[2] // HEAD_WIDTH
    key_rows = k_piece[0].reshape(tally_count, heads, HEAD_WIDTH)
    value_rows = v_piece[0].reshape(tally_count, heads, HEAD_WIDTH)
    k_positions = key_positions(tally_count, span_order, half)
    block = math.gcd(tally_count, 512)
    steps = tally_count // block

    def step_fn(state, items):
        return (update(query_rows, q_positions, state, items[0], items[1], items[2]), None)

    carry, unused = lax.scan(
        step_fn,
        carry,
        (
            key_rows.reshape(steps, block, heads, HEAD_WIDTH),
            value_rows.reshape(steps, block, heads, HEAD_WIDTH),
            k_positions.reshape(steps, block),
        ),
    )
    return carry


def blank_state(heads, query_group, row_indices):
    return (
        jnp.full((heads, query_group, row_indices), -1e30, jnp.float32),
        jnp.zeros((heads, query_group, row_indices), jnp.float32),
        jnp.zeros((row_indices, heads, query_group, HEAD_WIDTH), jnp.float32),
    )


def attention(query_previous, key_previous, value_previous, span_order):
    row_indices = query_previous.shape[1]
    half = row_indices // 2
    query_group = QUERY_HEADS // KEY_VALUE_HEADS
    mine = lax.dynamic_slice_in_dim(span_order, 2 * lax.axis_index("ctx"), 2)
    local = jnp.arange(row_indices, dtype=jnp.int32)
    q_positions = jnp.where(local < half, mine[0], mine[1]) * half + local % half
    query_rows = query_previous[0].reshape(row_indices, KEY_VALUE_HEADS, query_group, HEAD_WIDTH)
    top, total, summed = fold_piece(
        query_rows,
        q_positions,
        blank_state(KEY_VALUE_HEADS, query_group, row_indices),
        lax.all_gather(key_previous, "ctx", axis=1, tiled=True),
        lax.all_gather(value_previous, "ctx", axis=1, tiled=True),
        span_order,
        half,
    )
    output = summed / jnp.transpose(total, (2, 0, 1))[..., None]
    out_prev = output.reshape(1, row_indices, QUERY_HEADS * HEAD_WIDTH).astype(jnp.bfloat16)
    lse_prev = (top + jnp.log(total)).reshape(1, QUERY_HEADS, row_indices)
    return (out_prev, lse_prev)


def norm_backward(resid, grad_norm, gain):
    resid_f = resid[0].astype(jnp.float32)
    grad_f = grad_norm[0].astype(jnp.float32)
    inv_rms = 1.0 / jnp.sqrt(jnp.mean(resid_f * resid_f, axis=-1, keepdims=True) + 1e-05)
    normed = resid_f * inv_rms
    partial_grad = jnp.sum(grad_f * normed, axis=0)
    gain_grad = lax.psum(partial_grad, ("ctx", "dp"))
    scaled = gain[None, :] * grad_f
    resid_grad = (
        (scaled - normed * jnp.mean(scaled * normed, axis=-1, keepdims=True)) * inv_rms
    ).astype(jnp.bfloat16)
    return (gain_grad, resid_grad[None])


def per_device(query_previous, key_previous, value_previous, span_order, resid, grad_norm, gain):
    out_prev, lse_prev = attention(query_previous, key_previous, value_previous, span_order)
    gain_grad, resid_grad = norm_backward(resid, grad_norm, gain)
    return (out_prev, lse_prev, resid_grad, gain_grad)


def solution(mesh):
    return jax.shard_map(
        per_device,
        mesh=mesh,
        in_specs=(
            P("dp", "ctx", None),
            P("dp", "ctx", None),
            P("dp", "ctx", None),
            P(),
            P("dp", "ctx", None),
            P("dp", "ctx", None),
            P(),
        ),
        out_specs=(P("dp", "ctx", None), P("dp", None, "ctx"), P("dp", "ctx", None), P()),
        check_vma=False,
    )
```

profile of v0, /device:TPU:0, one launch (start us, length us, event | category | flops | bytes accessed | tf_op | source)
XLA Modules:
  0.0 89.5 jit_solution(13001923617092184318)
XLA Ops:
  7.2 0.7 all-gather.3.cloned.1.call-update
  8.0 0.7 all-gather.5.cloned.1.call-update
  8.7 0.7 dynamic_slice.27
  9.4 0.6 fusion.49
  10.0 1.3 %copy.20 = bf16[1,128,2048]{1,2,0:T(8,128)(2,1)S(1)} copy(bf16[1,128,2048]{2,1,0:T(8,128)(2,1)} %param.11) | data formatting | bytes 1048576 | tf_op args[0]
  11.3 0.3 copy.22
  11.6 0.7 select_reduce_fusion
  12.4 1.5 %fusion.38 = f32[128]{0:T(128)S(1)} fusion(bf16[1,128,4096]{2,1,0:T(8,128)(2,1)} %param.15), kind=kLoop, calls=%fused_computation.45 | loop fusion | flops 1572736 | bytes 1049088 | tf_op jit(solution)/shard_map/reduce_sum | solution.py:108
  13.9 1.9 %fusion.47 = s32[]{:T(128)} fusion(s32[]{:T(128)} %bitcast.11, s32[]{:T(128)} %bitcast.10), kind=kLoop, calls=%fused_computation.69 | loop fusion | flops 1407 | bytes 12 | tf_op jit(solution)/shard_map/while/body/eval_jaxpr/reduce_max | solution.py:39
  15.9 2.4 %fusion.34 = (f32[4096]{0:T(1024)S(1)}, f32[128]{0:T(128)S(1)}) fusion(bf16[1,128,4096]{2,1,0:T(8,128)(2,1)} %param.15, bf16[1,128,4096]{2,1,0:T(8,128)(2,1)} %param.16, f32[128]{0:T(128)S(1)} %add_rsqrt_fusion, f32[4096]{0:T(1024)} %param.17), kind=kLoop, calls=%fused_computation.41 | loop fusion | flops 4190080 | bytes 2130944 | tf_op jit(solution)/shard_map/reduce_sum | solution.py:110
  18.2 42.2 %psum.7 = f32[4096]{0:T(1024)} all-reduce(f32[4096]{0:T(1024)S(1)} %get-tuple-element.291), channel_id=1, replica_groups=mesh['ctx'=8,'dp'=4] {'ctx','dp'}, use_global_device_ids=true, to_apply=%region_12.13 | all-reduce | flops 4096 | bytes 32768 | tf_op jit(solution)/shard_map/psum | solution.py:111
  60.5 1.5 %fusion.37 = bf16[1,128,4096]{2,1,0:T(8,128)(2,1)} fusion(bf16[1,128,4096]{2,1,0:T(8,128)(2,1)S(1)} %copy-done.1, bf16[1,128,4096]{2,1,0:T(8,128)(2,1)S(1)} %copy-done, f32[128]{0:T(128)S(1)} %broadcast_multiply_fusion.1, f32[128]{0:T(128)S(1)} %add_rsqrt_fusion, f32[4096]{0:T(1024)S(1)} %copy-done.3), kind=kLoop, calls=%fused_computation.44 | loop fusion | flops 4194304 | bytes 3163136 | tf_op jit(solution)/shard_map/convert_element_type | solution.py:115
  62.0 1.3 %reshape_reshape_squeeze.6 = bf16[2,512,4,128]{3,2,1,0:T(4,128)(2,1)S(1)} reshape(bf16[1,1024,512]{2,1,0:T(8,128)(2,1)} %all-gather.3.cloned.1.call-done) | data formatting | bytes 2097152 | tf_op jit(solution)/shard_map/reshape;reshape;squeeze | solution.py:66
  63.5 1.3 %reshape_reshape_squeeze.7 = bf16[2,512,4,128]{3,2,1,0:T(4,128)(2,1)S(1)} reshape(bf16[1,1024,512]{2,1,0:T(8,128)(2,1)} %all-gather.5.cloned.1.call-done) | data formatting | bytes 2097152 | tf_op jit(solution)/shard_map/reshape;reshape;squeeze | solution.py:67
  64.9 1.1 %copy.23 = bf16[2,512,4,128]{3,1,2,0:T(8,128)(2,1)} copy(bf16[2,512,4,128]{3,2,1,0:T(4,128)(2,1)S(1)} %reshape_reshape_squeeze.7) | data formatting | bytes 2097152
  66.1 14.0 %while.16 = (s32[]{:T(128)}, f32[4,4,128]{2,1,0:T(4,128)S(1)}, f32[4,4,128]{2,1,0:T(4,128)S(1)}, f32[128,4,4,128]{3,0,2,1:T(8,128)S(1)}, s32[2,512]{1,0:T(2,128)...) while((s32[]{:T(128)}, f32[4,4,128]{2,1,0:T(4,128)S(1)}, ...), condition=%wide.region_8.9_spmd.clone, body=%wide.region_2.8_spmd.clone.sunk | while | flops 551100160 | bytes 20852624 | solution.py:62
  66.1 0.7 fusion.52
  68.2 5.0 %conditional.3 = ((f32[4,4,128]{2,1,0:T(4,128)S(1)}, f32[4,4,128]{2,1,0:T(4,128)S(1)}, f32[128,4,4,128]{3,0,2,1:T(8,128)S(1)})) conditional(s32[]{:T(128)} %convert_element_type.103, (s32[1,512]{1,0:T(1,128)S(1)}, s32[128]{0:T(128)S(1)}, bf16[2,512,4,128]{3,1,2,0:T(8,128)(2,1)S(1)}, s32[]{:T(128)}, bf16[128,4,4,128]{3,0,2,1:T(8,128)(2,1)S(1)}, ...), branch_computations={%region_4.6_spmd.clone, %region_7.7_spmd} | conditional | flops 551099520 | bytes 20846672 | solution.py:40
  68.2 1.3 %fusion.24 = s32[128]{0:T(128)S(1)} fusion(s32[128]{0:T(128)S(1)} %get-tuple-element.268, s32[128]{0:T(128)S(1)} %get-tuple-element.267, s32[128]{0:T(128)S(1)} %get-tuple-element.272, s32[128]{0:T(128)S(1)} %get-tuple-element.272, s32[128]{0:T(128)S(1)} %get-tuple-element.272, s32[128]{0:T(128)S(1)} %get-tuple-element.272, s32[]{:T(128)} %get-tuple-element.273, ...), kind=kLoop, calls=%fused_computation.25 | loop fusion | flops 1152 | bytes 3596 | tf_op jit(solution)/shard_map/add | solution.py:88
  69.6 0.8 fusion.2
  70.4 1.0 %fusion.4 = f32[4,4,128]{2,1,0:T(4,128)S(1)} fusion(f32[4,512,128,4]{2,1,3,0:T(8,128)S(1)} %get-tuple-element.320, f32[4,4,128]{2,1,0:T(4,128)S(1)} %get-tuple-element.400, pred[128,512]{0,1:T(8,128)(4,1)S(1)} %broadcast_compare_fusion), kind=kLoop, calls=%fused_computation.5 | loop fusion | flops 5240832 | bytes 4276224 | tf_op jit(solution)/shard_map/while/body/eval_jaxpr/cond/branch_0_fun/reduce_sum | solution.py:31
  71.4 1.7 %fusion.11 = f32[128,4,4,128]{3,0,2,1:T(8,128)S(1)} fusion(f32[4,512,128,4]{2,1,3,0:T(8,128)S(1)} %get-tuple-element.320, f32[4,4,128]{2,1,0:T(4,128)S(1)} %get-tuple-element.400, pred[128,512]{0,1:T(8,128)(4,1)S(1)} %broadcast_compare_fusion, f32[128,4,4,128]{3,0,2,1:T(8,128)S(1)} %get-tuple-element.261, bf16[2,512,4,128]{3,1,2,0:T(8,128)(2,1)S(1)} %copy-done.2, ...), kind=kOutput, calls=%fused_computation.9 | convolution fusion | flops 274202624 | bytes 6897668 | tf_op jit(solution)/shard_map/while/body/eval_jaxpr/cond/branch_0_fun/kgrs,skd->rkgd/dot_general | solution.py:33
  73.1 0.7 fusion.52
  75.2 5.0 %conditional.3 = ((f32[4,4,128]{2,1,0:T(4,128)S(1)}, f32[4,4,128]{2,1,0:T(4,128)S(1)}, f32[128,4,4,128]{3,0,2,1:T(8,128)S(1)})) conditional(s32[]{:T(128)} %convert_element_type.103, (s32[1,512]{1,0:T(1,128)S(1)}, s32[128]{0:T(128)S(1)}, bf16[2,512,4,128]{3,1,2,0:T(8,128)(2,1)S(1)}, s32[]{:T(128)}, bf16[128,4,4,128]{3,0,2,1:T(8,128)(2,1)S(1)}, ...), branch_computations={%region_4.6_spmd.clone, %region_7.7_spmd} | conditional | flops 551099520 | bytes 20846672 | solution.py:40
  75.2 1.3 %fusion.24 = s32[128]{0:T(128)S(1)} fusion(s32[128]{0:T(128)S(1)} %get-tuple-element.268, s32[128]{0:T(128)S(1)} %get-tuple-element.267, s32[128]{0:T(128)S(1)} %get-tuple-element.272, s32[128]{0:T(128)S(1)} %get-tuple-element.272, s32[128]{0:T(128)S(1)} %get-tuple-element.272, s32[128]{0:T(128)S(1)} %get-tuple-element.272, s32[]{:T(128)} %get-tuple-element.273, ...), kind=kLoop, calls=%fused_computation.25 | loop fusion | flops 1152 | bytes 3596 | tf_op jit(solution)/shard_map/add | solution.py:88
  76.6 0.8 fusion.2
  77.4 1.0 %fusion.4 = f32[4,4,128]{2,1,0:T(4,128)S(1)} fusion(f32[4,512,128,4]{2,1,3,0:T(8,128)S(1)} %get-tuple-element.320, f32[4,4,128]{2,1,0:T(4,128)S(1)} %get-tuple-element.400, pred[128,512]{0,1:T(8,128)(4,1)S(1)} %broadcast_compare_fusion), kind=kLoop, calls=%fused_computation.5 | loop fusion | flops 5240832 | bytes 4276224 | tf_op jit(solution)/shard_map/while/body/eval_jaxpr/cond/branch_0_fun/reduce_sum | solution.py:31
  78.4 1.7 %fusion.11 = f32[128,4,4,128]{3,0,2,1:T(8,128)S(1)} fusion(f32[4,512,128,4]{2,1,3,0:T(8,128)S(1)} %get-tuple-element.320, f32[4,4,128]{2,1,0:T(4,128)S(1)} %get-tuple-element.400, pred[128,512]{0,1:T(8,128)(4,1)S(1)} %broadcast_compare_fusion, f32[128,4,4,128]{3,0,2,1:T(8,128)S(1)} %get-tuple-element.261, bf16[2,512,4,128]{3,1,2,0:T(8,128)(2,1)S(1)} %copy-done.2, ...), kind=kOutput, calls=%fused_computation.9 | convolution fusion | flops 274202624 | bytes 6897668 | tf_op jit(solution)/shard_map/while/body/eval_jaxpr/cond/branch_0_fun/kgrs,skd->rkgd/dot_general | solution.py:33
  80.2 0.3 divide_convert_fusion
  80.5 0.4 copy.24
  80.9 1.2 %convert_element_type.46 = bf16[1,128,2048]{2,1,0:T(8,128)(2,1)} reshape(bf16[128,4,4,128]{3,2,1,0:T(4,128)(2,1)S(1)} %copy.24) | data formatting | bytes 1048576 | tf_op jit(solution)/shard_map/convert_element_type | solution.py:100
  82.1 0.6 log_add_fusion
  (38 shorter events, 0.7 us)
Async XLA Ops:
  7.2 53.3 %copy-start = (bf16[1,128,4096]{2,1,0:T(8,128)(2,1)S(1)}, bf16[1,128,4096]{2,1,0:T(8,128)(2,1)}, u32[]{:S(2)}) copy-start(bf16[1,128,4096]{2,1,0:T(8,128)(2,1)} %param.15) | copy-start | bytes 3145732
  7.2 53.3 %copy-start.1 = (bf16[1,128,4096]{2,1,0:T(8,128)(2,1)S(1)}, bf16[1,128,4096]{2,1,0:T(8,128)(2,1)}, u32[]{:S(2)}) copy-start(bf16[1,128,4096]{2,1,0:T(8,128)(2,1)} %param.16) | copy-start | bytes 3145732
  7.2 53.3 %copy-start.3 = (f32[4096]{0:T(1024)S(1)}, f32[4096]{0:T(1024)}, u32[]{:S(2)}) copy-start(f32[4096]{0:T(1024)} %param.17) | copy-start | bytes 49156
  7.2 54.8 %all-gather.3.cloned.1.call-start = ((), (), s32[]{:S(2)}) async-start(), calls=%async_computation | async-start | bytes 1179648 | tf_op jit(solution)/shard_map/all_gather | solution.py:94
  7.9 55.6 %all-gather.5.cloned.1.call-start = ((), (), s32[]{:S(2)}) async-start(), calls=%async_computation.1 | async-start | bytes 1179648 | tf_op jit(solution)/shard_map/all_gather | solution.py:95
  69.6 1.8 %copy-start.2 = (bf16[2,512,4,128]{3,1,2,0:T(8,128)(2,1)S(1)}, bf16[2,512,4,128]{3,1,2,0:T(8,128)(2,1)}, u32[]{:S(2)}) copy-start(bf16[2,512,4,128]{3,1,2,0:T(8,128)(2,1)} %get-tuple-element.262) | copy-start | bytes 3145732 | tf_op jit(solution)/shard_map/while/body/eval_jaxpr/cond
  76.6 1.8 %copy-start.2 = (bf16[2,512,4,128]{3,1,2,0:T(8,128)(2,1)S(1)}, bf16[2,512,4,128]{3,1,2,0:T(8,128)(2,1)}, u32[]{:S(2)}) copy-start(bf16[2,512,4,128]{3,1,2,0:T(8,128)(2,1)} %get-tuple-element.262) | copy-start | bytes 3145732 | tf_op jit(solution)/shard_map/while/body/eval_jaxpr/cond
Sparse Core Ops, SparseCore 0:
  9.9 26.1 all-gather.2
  38.0 23.9 all-gather.4
where the time goes:
time: 90.1 us; the launch traced here: 89.5 us
  blocking collectives  42.2 us (47%)
  other arithmetic  15.4 us (17%)
  between operations  14.2 us (16%)
  local copies, waits for them, and re-layouts  8.61 us (10%)
  matrix products  4.87 us (5%)
  loops' own time  2.82 us (3%)
  waiting for transfers between devices  1.4 us (2%)
    psum x1, blocking collectives, norm_backward(): gain_grad = lax.psum(partial_grad, ('ctx', 'dp'))  42.2 us
    dot_general x2, matrix products, dense_update(): jnp.einsum('kgrs,skd->rkgd', probs, value_rows, preferred_element_type=jn...  3.37 us
    unnamed x10, local copies, waits for them, and re-layouts  2.88 us
    another operation x1, loops' own time, fold_piece(): lax.scan(step_fn, carry, (key_rows.reshape(steps, block, heads, HEAD_WIDT...  2.66 us
    add x2, other arithmetic, attention(): jnp.where(local < half, mine[0], mine[1]) * half + local % half  2.54 us
    reduce_sum x1, other arithmetic, norm_backward(): partial_grad = jnp.sum(grad_f * normed, axis=0)  2.36 us
    reduce_sum x2, other arithmetic, dense_update(): total = total * factor + jnp.sum(weights, axis=-1)  2.02 us
    reduce_max x1, other arithmetic, update(): later = jnp.min(k_positions) > jnp.max(q_positions)  1.93 us
  transfers between devices with their start and end apart: 2, of which 0 were waited for; matrix products, arithmetic and copies ran while one was open for 14% of the time, Pallas kernels for 0%

commit v1 on v0

v1 whole, which is shorter than its diff:
```python
import functools
import math

import jax
import jax.numpy as jnp
from jax import lax
from jax.experimental import pallas as pl
from jax.experimental.pallas import tpu as pltpu
from jax.sharding import PartitionSpec as P

HEAD_WIDTH = 128
MESH = pl.DeviceIdType.MESH
LOW = -1e30


def kernel(
    n,
    dp_count,
    heads,
    kv_heads,
    q_hbm,
    k_hbm,
    v_hbm,
    span_hbm,
    resid_hbm,
    grad_hbm,
    gain_hbm,
    out_hbm,
    lse_hbm,
    rgrad_hbm,
    ggrad_hbm,
    k_all,
    v_all,
    q_buf,
    q_turned,
    spans,
    resid_buf,
    grad_buf,
    gain_buf,
    tops,
    totals,
    summed,
    out_buf,
    lse_buf,
    rgrad_buf,
    terms,
    part,
    part_in,
    level,
    whole,
    ggrad_buf,
    local_sem,
    kv_send,
    kv_recv,
    p1_send,
    p1_recv,
    p2_send,
    p2_recv,
    p3_send,
    p3_recv,
):
    rows = q_hbm.shape[0]
    width = resid_hbm.shape[1]
    half = rows // 2
    group = heads // kv_heads
    chips = n // 2
    piece = width // n
    span_count = span_hbm.shape[0]
    me = lax.axis_index("ctx")
    mine_dp = lax.axis_index("dp")
    chip = me // 2
    core = me % 2
    sibling = chip * 2 + (1 - core)
    square = chips == 4

    def other_chip(k):
        if square:
            low, high = chip % 2, chip // 2
            low = 1 - low if k % 2 else low
            high = 1 - high if k // 2 else high
            return high * 2 + low
        return (chip + k) % chips

    def ctx_peer(k):
        return (me + k) % n

    def dp_peer(k):
        return (mine_dp + k) % dp_count

    barrier = pltpu.get_barrier_semaphore()
    for k in range(1, n):
        pl.semaphore_signal(barrier, inc=1, device_id={"ctx": ctx_peer(k)}, device_id_type=MESH)
    for k in range(1, dp_count):
        pl.semaphore_signal(barrier, inc=1, device_id={"dp": dp_peer(k)}, device_id_type=MESH)

    def slot(ref, index, count=1):
        return ref.at[pl.ds(pl.multiple_of(index * rows, rows), count * rows), :]

    own_k = pltpu.make_async_copy(k_hbm, slot(k_all, me), local_sem.at[0])
    own_v = pltpu.make_async_copy(v_hbm, slot(v_all, me), local_sem.at[1])
    get_resid = pltpu.make_async_copy(resid_hbm, resid_buf, local_sem.at[2])
    get_grad = pltpu.make_async_copy(grad_hbm, grad_buf, local_sem.at[3])
    get_gain = pltpu.make_async_copy(gain_hbm, gain_buf, local_sem.at[4])
    get_span = pltpu.make_async_copy(span_hbm, spans, local_sem.at[5])
    get_q = pltpu.make_async_copy(q_hbm, q_buf, local_sem.at[6])
    for copy in (own_k, own_v, get_resid, get_grad, get_gain, get_span, get_q):
        copy.start()

    k_or_v = (k_all, v_all)
    source = (k_hbm, v_hbm)
    sends = []

    def send(which, index, target, lane, first=False):
        src = source[which] if first else slot(k_or_v[which], index)
        copy = pltpu.make_async_remote_copy(
            src_ref=src,
            dst_ref=slot(k_or_v[which], index),
            send_sem=kv_send.at[which, lane],
            recv_sem=kv_recv.at[which, index],
            device_id={"ctx": target},
            device_id_type=MESH,
        )
        copy.start()
        sends.append(copy)

    def arrived(which, index):
        pltpu.make_async_remote_copy(
            src_ref=slot(k_or_v[which], index),
            dst_ref=slot(k_or_v[which], index),
            send_sem=kv_send.at[which, 0],
            recv_sem=kv_recv.at[which, index],
            device_id={"ctx": sibling},
            device_id_type=MESH,
        ).wait_recv()

    pl.semaphore_wait(barrier, n - 1 + dp_count - 1)

    if square:
        send(0, me, other_chip(1) * 2 + core, 1, True)
        send(1, me, other_chip(2) * 2 + core, 2, True)
        send(1, me, other_chip(1) * 2 + core, 1, True)
        send(0, me, other_chip(2) * 2 + core, 2, True)
    else:
        for k in range(1, chips):
            send(0, me, other_chip(k) * 2 + core, k, True)
            send(1, me, other_chip(k) * 2 + core, k, True)
    send(0, me, sibling, 0, True)
    send(1, me, sibling, 0, True)

    get_resid.wait()
    get_grad.wait()
    get_gain.wait()
    tile, cols = 16, 512
    terms[...] = jnp.zeros_like(terms)

    def norm_rows(step, carry):
        at = pl.ds(pl.multiple_of(step * tile, tile), tile)
        squares = jnp.zeros((tile, cols), jnp.float32)
        products = jnp.zeros((tile, cols), jnp.float32)
        for c in range(0, width, cols):
            r = resid_buf[at, c : c + cols].astype(jnp.float32)
            g = grad_buf[at, c : c + cols].astype(jnp.float32)
            squares = squares + r * r
            products = products + gain_buf[:, c : c + cols] * g * r
        mean_square = jnp.sum(squares, axis=1, keepdims=True) * (1.0 / width)
        inv = 1.0 / jnp.sqrt(mean_square + 1e-05)
        mean_product = jnp.sum(products, axis=1, keepdims=True) * inv * (1.0 / width)
        for c in range(0, width, cols):
            r = resid_buf[at, c : c + cols].astype(jnp.float32)
            g = grad_buf[at, c : c + cols].astype(jnp.float32)
            normed = r * inv
            term = g * normed
            terms[:, c : c + cols] += term[:8] + term[8:]
            scaled = gain_buf[:, c : c + cols] * g
            rgrad_buf[at, c : c + cols] = ((scaled - normed * mean_product) * inv).astype(
                rgrad_buf.dtype
            )
        return carry

    lax.fori_loop(0, rows // tile, norm_rows, 0)
    put_rgrad = pltpu.make_async_copy(rgrad_buf, rgrad_hbm, local_sem.at[7])
    put_rgrad.start()
    for r in range(n):
        part[r] = jnp.sum(terms[:, r * piece : (r + 1) * piece], axis=0, keepdims=True)

    get_q.wait()
    for h in range(heads):
        turned = jnp.transpose(q_buf[:, h * HEAD_WIDTH : (h + 1) * HEAD_WIDTH])
        q_turned[h // group, :, (h % group) * rows : (h % group + 1) * rows] = turned

    p1 = []
    for k in range(1, n):
        peer = ctx_peer(k)
        copy = pltpu.make_async_remote_copy(
            src_ref=part.at[peer],
            dst_ref=part_in.at[me],
            send_sem=p1_send.at[k],
            recv_sem=p1_recv.at[k],
            device_id={"ctx": peer},
            device_id_type=MESH,
        )
        copy.start()
        p1.append(copy)
    part_in[me] = part[me]

    get_span.wait()
    lane = lax.broadcasted_iota(jnp.int32, (1, rows), 1)
    q_pos = (
        jnp.where(lane < half, spans[2 * me], spans[2 * me + 1]) * half + lane % half
    )
    scale = HEAD_WIDTH ** (-0.5)
    exponent = scale * math.log2(math.e)

    def fold(other, first):
        line = lax.broadcasted_iota(jnp.int32, (2 * rows, 1), 0)
        base = jnp.full((2 * rows, 1), spans[4 * other], jnp.int32)
        for i in range(1, 4):
            base = jnp.where(line >= i * half, spans[4 * other + i], base)
        k_pos = base * half + line % half
        bias = jnp.where(k_pos <= q_pos, 0.0, LOW)
        at = pl.ds(pl.multiple_of(other * 2 * rows, 2 * rows), 2 * rows)
        for h in range(kv_heads):
            band = slice(h * HEAD_WIDTH, (h + 1) * HEAD_WIDTH)
            scores = jnp.dot(k_all[at, band], q_turned[h], preferred_element_type=jnp.float32)
            probs, factors = [], []
            for g in range(group):
                lanes = slice(g * rows, (g + 1) * rows)
                s = scores[:, lanes] + bias
                top = jnp.max(s, axis=0, keepdims=True)
                if not first:
                    before = tops[h : h + 1, lanes]
                    top = jnp.maximum(top, before)
                    factor = jnp.exp2((before - top) * exponent)
                    factors.append(factor)
                w = jnp.exp2((s - top) * exponent)
                total = jnp.sum(w, axis=0, keepdims=True)
                if not first:
                    total = total + totals[h : h + 1, lanes] * factor
                tops[h : h + 1, lanes] = top
                totals[h : h + 1, lanes] = total
                probs.append(w.astype(jnp.bfloat16))
            added = lax.dot_general(
                v_all[at, band],
                jnp.concatenate(probs, axis=1),
                (((0,), (0,)), ((), ())),
                preferred_element_type=jnp.float32,
            )
            if first:
                summed[h] = added
            else:
                summed[h] = summed[h] * jnp.concatenate(factors, axis=1) + added

    own_k.wait()
    own_v.wait()
    arrived(0, sibling)
    arrived(1, sibling)
    fold(chip, True)

    def gain_two():
        for copy in p1:
            copy.wait()
        level[mine_dp] = jnp.sum(part_in[...], axis=0)
        copies = []
        for k in range(1, dp_count):
            copy = pltpu.make_async_remote_copy(
                src_ref=level.at[mine_dp],
                dst_ref=level.at[mine_dp],
                send_sem=p2_send.at[k],
                recv_sem=p2_recv.at[k],
                device_id={"dp": dp_peer(k)},
                device_id_type=MESH,
            )
            copy.start()
            copies.append(copy)
        return copies

    def gain_three(copies):
        for copy in copies:
            copy.wait()
        whole[me] = jnp.sum(level[...], axis=0)
        copies = []
        for k in range(1, n):
            copy = pltpu.make_async_remote_copy(
                src_ref=whole.at[me],
                dst_ref=whole.at[me],
                send_sem=p3_send.at[k],
                recv_sem=p3_recv.at[k],
                device_id={"ctx": ctx_peer(k)},
                device_id_type=MESH,
            )
            copy.start()
            copies.append(copy)
        return copies

    if square:
        near, far, across = other_chip(1), other_chip(2), other_chip(3)
        near_c, far_c, across_c = near * 2 + core, far * 2 + core, across * 2 + core
        arrived(0, near_c)
        send(0, near_c, far_c, 3)
        send(0, near_c, sibling, 4)
        arrived(1, far_c)
        send(1, far_c, near_c, 3)
        send(1, far_c, sibling, 4)
        p2 = gain_two()
        arrived(1, near_c)
        send(1, near_c, sibling, 5)
        arrived(0, far_c)
        send(0, far_c, sibling, 5)
        for other in (near, far):
            arrived(0, other * 2 + 1 - core)
            arrived(1, other * 2 + 1 - core)
            fold(other, False)
        p3 = gain_three(p2)
        arrived(0, across_c)
        send(0, across_c, sibling, 6)
        arrived(1, across_c)
        send(1, across_c, sibling, 6)
        arrived(0, across * 2 + 1 - core)
        arrived(1, across * 2 + 1 - core)
        fold(across, False)
    else:
        p2 = gain_two()
        p3 = gain_three(p2)

        def step(k, carry):
            other = (chip + chips - k) % chips
            held = other * 2 + core
            for which in range(2):
                arrived(which, held)
                copy = pltpu.make_async_remote_copy(
                    src_ref=slot(k_or_v[which], held),
                    dst_ref=slot(k_or_v[which], held),
                    send_sem=kv_send.at[which, chips],
                    recv_sem=kv_recv.at[which, held],
                    device_id={"ctx": sibling},
                    device_id_type=MESH,
                )
                copy.start()
                arrived(which, other * 2 + 1 - core)
                copy.wait_send()
            fold(other, False)
            return carry

        lax.fori_loop(1, chips, step, 0)

    for h in range(heads):
        lanes = slice((h % group) * rows, (h % group + 1) * rows)
        kv = h // group
        total = totals[kv : kv + 1, lanes]
        lse_buf[h : h + 1, :] = tops[kv : kv + 1, lanes] * scale + jnp.log(total)
        out_buf[:, h * HEAD_WIDTH : (h + 1) * HEAD_WIDTH] = jnp.transpose(
            summed[kv, :, lanes] * (1.0 / total)
        ).astype(out_buf.dtype)
    put_out = pltpu.make_async_copy(out_buf, out_hbm, local_sem.at[8])
    put_out.start()
    put_lse = pltpu.make_async_copy(lse_buf, lse_hbm, local_sem.at[9])
    put_lse.start()
    for copy in p3:
        copy.wait()
    for r in range(n):
        ggrad_buf[:, r * piece : (r + 1) * piece] = whole[r]
    put_ggrad = pltpu.make_async_copy(ggrad_buf, ggrad_hbm, local_sem.at[10])
    put_ggrad.start()
    for copy in sends:
        copy.wait_send()
    for copy in (put_rgrad, put_out, put_lse, put_ggrad):
        copy.wait()


def per_device(n, dp_count, query, key, value, span_order, resid, grad_norm, gain):
    rows, q_width = query.shape[1:]
    kv_width = key.shape[2]
    width = resid.shape[2]
    heads, kv_heads = q_width // HEAD_WIDTH, kv_width // HEAD_WIDTH
    group = heads // kv_heads
    piece = width // n
    f32, bf16 = jnp.float32, jnp.bfloat16
    dma = pltpu.SemaphoreType.DMA
    lanes = max(8, n // 2 + 1)
    out, lse, rgrad, ggrad = pl.pallas_call(
        functools.partial(kernel, n, dp_count, heads, kv_heads),
        out_shape=(
            jax.ShapeDtypeStruct((rows, q_width), bf16),
            jax.ShapeDtypeStruct((heads, rows), f32),
            jax.ShapeDtypeStruct((rows, width), bf16),
            jax.ShapeDtypeStruct((1, width), f32),
        ),
        in_specs=[pl.BlockSpec(memory_space=pl.ANY)] * 7,
        out_specs=[pl.BlockSpec(memory_space=pl.ANY)] * 4,
        scratch_shapes=[
            pltpu.VMEM((n * rows, kv_width), bf16),
            pltpu.VMEM((n * rows, kv_width), bf16),
            pltpu.VMEM((rows, q_width), bf16),
            pltpu.VMEM((kv_heads, HEAD_WIDTH, group * rows), bf16),
            pltpu.SMEM(span_order.shape, jnp.int32),
            pltpu.VMEM((rows, width), bf16),
            pltpu.VMEM((rows, width), bf16),
            pltpu.VMEM((1, width), f32),
            pltpu.VMEM((kv_heads, group * rows), f32),
            pltpu.VMEM((kv_heads, group * rows), f32),
            pltpu.VMEM((kv_heads, HEAD_WIDTH, group * rows), f32),
            pltpu.VMEM((rows, q_width), bf16),
            pltpu.VMEM((heads, rows), f32),
            pltpu.VMEM((rows, width), bf16),
            pltpu.VMEM((8, width), f32),
            pltpu.VMEM((n, 1, piece), f32),
            pltpu.VMEM((n, 1, piece), f32),
            pltpu.VMEM((dp_count, 1, piece), f32),
            pltpu.VMEM((n, 1, piece), f32),
            pltpu.VMEM((1, width), f32),
            dma((11,)),
            dma((2, lanes)),
            dma((2, n)),
            dma((n,)),
            dma((n,)),
            dma((dp_count,)),
            dma((dp_count,)),
            dma((n,)),
            dma((n,)),
        ],
        compiler_params=pltpu.CompilerParams(collective_id=0, has_side_effects=True),
    )(
        query[0],
        key[0],
        value[0],
        span_order,
        resid[0],
        grad_norm[0],
        gain[None, :],
    )
    return (out[None], lse[None], rgrad[None], ggrad[0])


def solution(mesh):
    return jax.shard_map(
        functools.partial(per_device, mesh.shape["ctx"], mesh.shape["dp"]),
        mesh=mesh,
        in_specs=(
            P("dp", "ctx", None),
            P("dp", "ctx", None),
            P("dp", "ctx", None),
            P(),
            P("dp", "ctx", None),
            P("dp", "ctx", None),
            P(),
        ),
        out_specs=(P("dp", "ctx", None), P("dp", None, "ctx"), P("dp", "ctx", None), P()),
        check_vma=False,
    )
```

time: 90.1 us -> 28.7 us (0.32)
  blocking collectives: 42.2 us -> 0 us
  Pallas kernels: 0 us -> 23.7 us
  other arithmetic: 15.4 us -> 0 us
  between operations: 14.2 us -> 0.66 us
  matrix products: 4.87 us -> 0 us
  local copies, waits for them, and re-layouts: 8.61 us -> 4.16 us
  loops' own time: 2.82 us -> 0 us
  waiting for transfers between devices: 1.4 us -> 0 us
    psum x1 -> x0, blocking collectives: 42.2 us -> none  [norm_backward(): gain_grad = lax.psum(partial_grad, ('ctx', 'dp'))]
    pallas_call x0 -> x1, Pallas kernels: none -> 23.7 us  [per_device(): pl.pallas_call(functools.partial(kernel, n, dp_count, heads, kv_heads), o...]
    reduce_sum x5 -> x0, other arithmetic: 6.64 us -> none  [the longest x1 2.36 us: norm_backward(): partial_grad = jnp.sum(grad_f * normed, axis=0)]
    dot_general x4 -> x0, matrix products: 4.87 us -> none  [the longest x2 3.37 us: dense_update(): jnp.einsum('kgrs,skd->rkgd', probs, value_rows, preferred_element_type=jn...]
    add x6 -> x0, other arithmetic: 3.18 us -> none  [the longest x2 2.54 us: attention(): jnp.where(local < half, mine[0], mine[1]) * half + local % half]
    another operation x3 -> x0, loops' own time: 2.82 us -> none  [the longest x1 2.66 us: fold_piece(): lax.scan(step_fn, carry, (key_rows.reshape(steps, block, heads, HEAD_WIDT...]
    another operation x4 -> x0, local copies, waits for them, and re-layouts: 2.69 us -> none  [the longest x1 1.35 us: fold_piece(): value_rows.reshape(steps, block, heads, HEAD_WIDTH)]
    reduce_max x1 -> x0, other arithmetic: 1.93 us -> none  [update(): later = jnp.min(k_positions) > jnp.max(q_positions)]
  transfers between devices with their start and end apart: 2 -> 0, of which waited for: 0 -> 0; matrix products, arithmetic and copies ran while one was open for 14% -> 0% of each run, Pallas kernels for 0% -> 0%
where the time goes in v1:
time: 28.7 us; the launch traced here: 28.6 us
  Pallas kernels  23.7 us (83%)
  local copies, waits for them, and re-layouts  4.16 us (14%)
  between operations  0.66 us (2%)
    pallas_call x1, Pallas kernels, per_device(): pl.pallas_call(functools.partial(kernel, n, dp_count, heads, kv_heads), o...  23.7 us
    unnamed x10, local copies, waits for them, and re-layouts  4.16 us

profile of v1, /device:TPU:0, one launch (start us, length us, event | category | flops | bytes accessed | tf_op | source)
XLA Modules:
  0.0 28.6 jit_solution(1158350172321042304)
XLA Ops:
  0.6 23.7 %shard_map.102 = (bf16[128,2048]{1,0:T(8,128)(2,1)}, f32[16,128]{1,0:T(8,128)}, bf16[128,4096]{1,0:T(8,128)(2,1)}, f32[1,4096]{1,0:T(1,128)}) custom-call(bf16[128,2048]{1,0:T(8,128)(2,1)} %bitcast.13, bf16[128,512]{1,0:T(8,128)(2,1)} %bitcast.15, bf16[128,512]{1,0:T(8,128)(2,1)} %bitcast.16, s32[16]{0:T(128)} %span_hbm.1, bf16[128,4096]{1,0:T(8,128)(2,1)} %bitcast.10, ...), custom_call_target="tpu_custom_call" | custom-call | tf_op jit(solution)/shard_map/pallas_call | solution.py:380
  24.4 0.0 copy-start
  24.4 0.0 copy-start.2
  24.4 2.0 %copy.15 = bf16[1,128,2048]{2,1,0:T(8,128)(2,1)} copy(bf16[1,128,2048]{2,1,0:T(8,128)(2,1)} %bitcast.14) | data formatting | bytes 1048576
  26.4 0.0 copy-done.2
  26.4 0.6 %copy.16 = f32[1,16,128]{2,1,0:T(8,128)} copy(f32[1,16,128]{2,1,0:T(8,128)S(1)} %bitcast.19) | data formatting | bytes 16384
  27.0 0.0 copy-done
  27.0 0.0 copy-start.1
  27.0 1.0 %copy.17 = bf16[1,128,4096]{2,1,0:T(8,128)(2,1)} copy(bf16[1,128,4096]{2,1,0:T(8,128)(2,1)S(1)} %bitcast.12) | data formatting | bytes 2097152
  28.0 0.0 copy-done.1
  28.0 0.6 %copy.18 = f32[4096]{0:T(1024)} copy(f32[4096]{0:T(1024)S(1)} %bitcast.18) | data formatting | bytes 32768
Async XLA Ops:
  24.4 2.6 %copy-start = (bf16[128,4096]{1,0:T(8,128)(2,1)S(1)}, bf16[128,4096]{1,0:T(8,128)(2,1)}, u32[]{:S(2)}) copy-start(bf16[128,4096]{1,0:T(8,128)(2,1)} %get-tuple-element.10) | copy-start | bytes 3145732
  24.4 2.0 %copy-start.2 = (f32[16,128]{1,0:T(8,128)S(1)}, f32[16,128]{1,0:T(8,128)}, u32[]{:S(2)}) copy-start(f32[16,128]{1,0:T(8,128)} %get-tuple-element.9) | copy-start | bytes 24580
  27.0 1.0 %copy-start.1 = (f32[1,4096]{1,0:T(1,128)S(1)}, f32[1,4096]{1,0:T(1,128)}, u32[]{:S(2)}) copy-start(f32[1,4096]{1,0:T(1,128)} %get-tuple-element.11) | copy-start | bytes 49156

commit v2 on v1

--- a/solution.py
+++ b/solution.py
@@ -25,10 +25,11 @@
     resid_hbm,
     grad_hbm,
     gain_hbm,
-    out_hbm,
-    lse_hbm,
-    rgrad_hbm,
-    ggrad_hbm,
+    summed,
+    tops,
+    totals,
+    rgrad_buf,
+    ggrad_buf,
     k_all,
     v_all,
     q_buf,
@@ -37,18 +38,11 @@
     resid_buf,
     grad_buf,
     gain_buf,
-    tops,
-    totals,
-    summed,
-    out_buf,
-    lse_buf,
-    rgrad_buf,
     terms,
     part,
     part_in,
     level,
     whole,
-    ggrad_buf,
     local_sem,
     kv_send,
     kv_recv,
@@ -178,8 +172,6 @@
         return carry
 
     lax.fori_loop(0, rows // tile, norm_rows, 0)
-    put_rgrad = pltpu.make_async_copy(rgrad_buf, rgrad_hbm, local_sem.at[7])
-    put_rgrad.start()
     for r in range(n):
         part[r] = jnp.sum(terms[:, r * piece : (r + 1) * piece], axis=0, keepdims=True)
 
@@ -343,27 +335,43 @@
 
         lax.fori_loop(1, chips, step, 0)
 
-    for h in range(heads):
-        lanes = slice((h % group) * rows, (h % group + 1) * rows)
-        kv = h // group
-        total = totals[kv : kv + 1, lanes]
-        lse_buf[h : h + 1, :] = tops[kv : kv + 1, lanes] * scale + jnp.log(total)
-        out_buf[:, h * HEAD_WIDTH : (h + 1) * HEAD_WIDTH] = jnp.transpose(
-            summed[kv, :, lanes] * (1.0 / total)
-        ).astype(out_buf.dtype)
-    put_out = pltpu.make_async_copy(out_buf, out_hbm, local_sem.at[8])
-    put_out.start()
-    put_lse = pltpu.make_async_copy(lse_buf, lse_hbm, local_sem.at[9])
-    put_lse.start()
     for copy in p3:
         copy.wait()
     for r in range(n):
         ggrad_buf[:, r * piece : (r + 1) * piece] = whole[r]
-    put_ggrad = pltpu.make_async_copy(ggrad_buf, ggrad_hbm, local_sem.at[10])
-    put_ggrad.start()
     for copy in sends:
         copy.wait_send()
-    for copy in (put_rgrad, put_out, put_lse, put_ggrad):
+
+def finish(
+    heads, kv_heads, summed, tops, totals, rgrad, ggrad,
+    out_hbm, lse_hbm, rgrad_hbm, ggrad_hbm, out_buf, lse_buf, sem
+):
+    rows = out_hbm.shape[0]
+    group = heads // kv_heads
+    scale = HEAD_WIDTH ** (-0.5)
+    puts = [
+        pltpu.make_async_copy(rgrad, rgrad_hbm, sem.at[0]),
+        pltpu.make_async_copy(ggrad, ggrad_hbm, sem.at[1]),
+    ]
+    for copy in puts:
+        copy.start()
+    for kv in range(kv_heads):
+        for g in range(group):
+            h = kv * group + g
+            lanes = slice(g * rows, (g + 1) * rows)
+            total = totals[kv : kv + 1, lanes]
+            lse_buf[h : h + 1, :] = tops[kv : kv + 1, lanes] * scale + jnp.log(total)
+            out_buf[:, h * HEAD_WIDTH : (h + 1) * HEAD_WIDTH] = jnp.transpose(
+                summed[kv, :, lanes] * (1.0 / total)
+            ).astype(out_buf.dtype)
+        band = pl.ds(kv * group * HEAD_WIDTH, group * HEAD_WIDTH)
+        copy = pltpu.make_async_copy(out_buf.at[:, band], out_hbm.at[:, band], sem.at[3 + kv])
+        copy.start()
+        puts.append(copy)
+    copy = pltpu.make_async_copy(lse_buf, lse_hbm, sem.at[2])
+    copy.start()
+    puts.append(copy)
+    for copy in puts:
         copy.wait()
 
 
@@ -377,16 +385,19 @@
     f32, bf16 = jnp.float32, jnp.bfloat16
     dma = pltpu.SemaphoreType.DMA
     lanes = max(8, n // 2 + 1)
-    out, lse, rgrad, ggrad = pl.pallas_call(
+    middle = (
+        pltpu.VMEM((kv_heads, HEAD_WIDTH, group * rows), f32),
+        pltpu.VMEM((kv_heads, group * rows), f32),
+        pltpu.VMEM((kv_heads, group * rows), f32),
+        pltpu.VMEM((rows, width), bf16),
+        pltpu.VMEM((1, width), f32),
+    )
+    vmem = pl.BlockSpec(memory_space=pltpu.VMEM)
+    results = pl.pallas_call(
         functools.partial(kernel, n, dp_count, heads, kv_heads),
-        out_shape=(
-            jax.ShapeDtypeStruct((rows, q_width), bf16),
-            jax.ShapeDtypeStruct((heads, rows), f32),
-            jax.ShapeDtypeStruct((rows, width), bf16),
-            jax.ShapeDtypeStruct((1, width), f32),
-        ),
+        out_shape=middle,
         in_specs=[pl.BlockSpec(memory_space=pl.ANY)] * 7,
-        out_specs=[pl.BlockSpec(memory_space=pl.ANY)] * 4,
+        out_specs=[vmem] * 5,
         scratch_shapes=[
             pltpu.VMEM((n * rows, kv_width), bf16),
             pltpu.VMEM((n * rows, kv_width), bf16),
@@ -396,19 +407,12 @@
             pltpu.VMEM((rows, width), bf16),
             pltpu.VMEM((rows, width), bf16),
             pltpu.VMEM((1, width), f32),
-            pltpu.VMEM((kv_heads, group * rows), f32),
-            pltpu.VMEM((kv_heads, group * rows), f32),
-            pltpu.VMEM((kv_heads, HEAD_WIDTH, group * rows), f32),
-            pltpu.VMEM((rows, q_width), bf16),
-            pltpu.VMEM((heads, rows), f32),
-            pltpu.VMEM((rows, width), bf16),
             pltpu.VMEM((8, width), f32),
             pltpu.VMEM((n, 1, piece), f32),
             pltpu.VMEM((n, 1, piece), f32),
             pltpu.VMEM((dp_count, 1, piece), f32),
             pltpu.VMEM((n, 1, piece), f32),
-            pltpu.VMEM((1, width), f32),
-            dma((11,)),
+            dma((7,)),
             dma((2, lanes)),
             dma((2, n)),
             dma((n,)),
@@ -428,6 +432,22 @@
         grad_norm[0],
         gain[None, :],
     )
+    out, lse, rgrad, ggrad = pl.pallas_call(
+        functools.partial(finish, heads, kv_heads),
+        out_shape=(
+            jax.ShapeDtypeStruct((rows, q_width), bf16),
+            jax.ShapeDtypeStruct((heads, rows), f32),
+            jax.ShapeDtypeStruct((rows, width), bf16),
+            jax.ShapeDtypeStruct((1, width), f32),
+        ),
+        in_specs=[vmem] * 5,
+        out_specs=[pl.BlockSpec(memory_space=pl.ANY)] * 4,
+        scratch_shapes=[
+            pltpu.VMEM((rows, q_width), bf16),
+            pltpu.VMEM((heads, rows), f32),
+            dma((3 + kv_heads,)),
+        ],
+    )(*(pltpu.with_memory_space_constraint(part, pltpu.VMEM) for part in results))
     return (out[None], lse[None], rgrad[None], ggrad[0])
 
 

time: 28.7 us -> 24.8 us (0.86)
  local copies, waits for them, and re-layouts: 4.16 us -> 0 us
  Pallas kernels: 23.7 us -> 24 us
    unnamed x10 -> x0, local copies, waits for them, and re-layouts: 4.16 us -> none
    pallas_call x0 -> x1, Pallas kernels: none -> 1.2 us  [per_device(): pl.pallas_call(functools.partial(finish, heads, kv_heads), out_shape=(jax...]
    pallas_call x1, Pallas kernels: 23.7 us -> 22.8 us  [per_device(): pl.pallas_call(functools.partial(kernel, n, dp_count, heads, kv_heads), o...]
where the time goes in v2:
time: 24.8 us; the launch traced here: 24.7 us
  Pallas kernels  24 us (97%)
  between operations  0.64 us (3%)
    pallas_call x1, Pallas kernels, per_device(): pl.pallas_call(functools.partial(kernel, n, dp_count, heads, kv_heads), o...  22.8 us
    pallas_call x1, Pallas kernels, per_device(): pl.pallas_call(functools.partial(finish, heads, kv_heads), out_shape=(jax...  1.2 us

profile of v2, /device:TPU:0, one launch (start us, length us, event | category | flops | bytes accessed | tf_op | source)
XLA Modules:
  0.0 24.7 jit_solution(41781538141205058)
XLA Ops:
  0.6 22.8 %shard_map.102 = (f32[4,128,512]{2,1,0:T(8,128)S(1)}, f32[4,512]{1,0:T(4,128)S(1)}, f32[4,512]{1,0:T(4,128)S(1)}, bf16[128,4096]{1,0:T(8,128)(2,1)S(1)}, f32[1,4096]{1,0:T(1,128)S(1)}) custom-call(bf16[128,2048]{1,0:T(8,128)(2,1)} %bitcast.12, bf16[128,512]{1,0:T(8,128)(2,1)} %bitcast.13, bf16[128,512]{1,0:T(8,128)(2,1)} %bitcast.14, s32[16]{0:T(128)} %span_hbm.1, ...), custom_call_target="tpu_custom_call" | custom-call | tf_op jit(solution)/shard_map/pallas_call | solution.py:396
  23.5 1.2 %shard_map.103 = (bf16[128,2048]{1,0:T(8,128)(2,1)}, f32[16,128]{1,0:T(8,128)}, bf16[128,4096]{1,0:T(8,128)(2,1)}, f32[1,4096]{1,0:T(1,128)}) custom-call(f32[4,128,512]{2,1,0:T(8,128)S(1)} %get-tuple-element.13.summed, f32[4,512]{1,0:T(4,128)S(1)} %get-tuple-element.14.tops, f32[4,512]{1,0:T(4,128)S(1)} %get-tuple-element.15.totals, ...), custom_call_target="tpu_custom_call" | custom-call | tf_op jit(solution)/shard_map/pallas_call | solution.py:435

commit v3 on v2

--- a/solution.py
+++ b/solution.py
@@ -42,6 +42,7 @@
     part,
     part_in,
     level,
+    cross,
     whole,
     local_sem,
     kv_send,
@@ -55,11 +56,12 @@
 ):
     rows = q_hbm.shape[0]
     width = resid_hbm.shape[1]
-    half = rows // 2
+    span = rows // 2
     group = heads // kv_heads
     chips = n // 2
-    piece = width // n
-    span_count = span_hbm.shape[0]
+    piece = width // 2
+    pair_heads = kv_heads // 2
+    cut = pair_heads * HEAD_WIDTH
     me = lax.axis_index("ctx")
     mine_dp = lax.axis_index("dp")
     chip = me // 2
@@ -75,15 +77,14 @@
             return high * 2 + low
         return (chip + k) % chips
 
-    def ctx_peer(k):
-        return (me + k) % n
-
     def dp_peer(k):
         return (mine_dp + k) % dp_count
 
     barrier = pltpu.get_barrier_semaphore()
-    for k in range(1, n):
-        pl.semaphore_signal(barrier, inc=1, device_id={"ctx": ctx_peer(k)}, device_id_type=MESH)
+    pl.semaphore_signal(barrier, inc=1, device_id={"ctx": sibling}, device_id_type=MESH)
+    for k in range(1, chips):
+        peer = other_chip(k) * 2 + core
+        pl.semaphore_signal(barrier, inc=1, device_id={"ctx": peer}, device_id_type=MESH)
     for k in range(1, dp_count):
         pl.semaphore_signal(barrier, inc=1, device_id={"dp": dp_peer(k)}, device_id_type=MESH)
 
@@ -104,30 +105,32 @@
     source = (k_hbm, v_hbm)
     sends = []
 
-    def send(which, index, target, lane, first=False):
-        src = source[which] if first else slot(k_or_v[which], index)
-        copy = pltpu.make_async_remote_copy(
-            src_ref=src,
-            dst_ref=slot(k_or_v[which], index),
-            send_sem=kv_send.at[which, lane],
-            recv_sem=kv_recv.at[which, index],
+    def part_of(ref, half, index):
+        at = pl.ds(pl.multiple_of(index * rows, rows), rows)
+        return ref.at[at, half * cut : (half + 1) * cut]
+
+    def carry(which, half, index, target, lane, first=False):
+        held = part_of(k_or_v[which], half, index)
+        return pltpu.make_async_remote_copy(
+            src_ref=source[which].at[:, half * cut : (half + 1) * cut] if first else held,
+            dst_ref=held,
+            send_sem=kv_send.at[which, half, lane],
+            recv_sem=kv_recv.at[which, half, index],
             device_id={"ctx": target},
             device_id_type=MESH,
         )
-        copy.start()
-        sends.append(copy)
-
-    def arrived(which, index):
-        pltpu.make_async_remote_copy(
-            src_ref=slot(k_or_v[which], index),
-            dst_ref=slot(k_or_v[which], index),
-            send_sem=kv_send.at[which, 0],
-            recv_sem=kv_recv.at[which, index],
-            device_id={"ctx": sibling},
-            device_id_type=MESH,
-        ).wait_recv()
-
-    pl.semaphore_wait(barrier, n - 1 + dp_count - 1)
+
+    def send(half, index, target, lane, first=False):
+        for which in range(2):
+            copy = carry(which, half, index, target, lane, first)
+            copy.start()
+            sends.append(copy)
+
+    def arrived(half, index):
+        for which in range(2):
+            carry(which, half, index, sibling, 0).wait_recv()
+
+    pl.semaphore_wait(barrier, chips + dp_count - 1)
 
     if square:
         send(0, me, other_chip(1) * 2 + core, 1, True)
@@ -136,10 +139,10 @@
         send(0, me, other_chip(2) * 2 + core, 2, True)
     else:
         for k in range(1, chips):
-            send(0, me, other_chip(k) * 2 + core, k, True)
-            send(1, me, other_chip(k) * 2 + core, k, True)
-    send(0, me, sibling, 0, True)
-    send(1, me, sibling, 0, True)
+            for half in range(2):
+                send(half, me, other_chip(k) * 2 + core, k, True)
+    for half in range(2):
+        send(half, me, sibling, 0, True)
 
     get_resid.wait()
     get_grad.wait()
@@ -172,46 +175,56 @@
         return carry
 
     lax.fori_loop(0, rows // tile, norm_rows, 0)
-    for r in range(n):
+    for r in range(2):
         part[r] = jnp.sum(terms[:, r * piece : (r + 1) * piece], axis=0, keepdims=True)
+
+    join = pltpu.make_async_remote_copy(
+        src_ref=part.at[1 - core],
+        dst_ref=part_in.at[0],
+        send_sem=p1_send.at[0],
+        recv_sem=p1_recv.at[0],
+        device_id={"ctx": sibling},
+        device_id_type=MESH,
+    )
+    join.start()
 
     get_q.wait()
     for h in range(heads):
         turned = jnp.transpose(q_buf[:, h * HEAD_WIDTH : (h + 1) * HEAD_WIDTH])
         q_turned[h // group, :, (h % group) * rows : (h % group + 1) * rows] = turned
 
-    p1 = []
-    for k in range(1, n):
-        peer = ctx_peer(k)
+    join.wait()
+    level[mine_dp] = part[core] + part_in[0]
+    over_dp = []
+    for k in range(1, dp_count):
         copy = pltpu.make_async_remote_copy(
-            src_ref=part.at[peer],
-            dst_ref=part_in.at[me],
-            send_sem=p1_send.at[k],
-            recv_sem=p1_recv.at[k],
-            device_id={"ctx": peer},
+            src_ref=level.at[mine_dp],
+            dst_ref=level.at[mine_dp],
+            send_sem=p2_send.at[k],
+            recv_sem=p2_recv.at[k],
+            device_id={"dp": dp_peer(k)},
             device_id_type=MESH,
         )
         copy.start()
-        p1.append(copy)
-    part_in[me] = part[me]
+        over_dp.append(copy)
 
     get_span.wait()
     lane = lax.broadcasted_iota(jnp.int32, (1, rows), 1)
     q_pos = (
-        jnp.where(lane < half, spans[2 * me], spans[2 * me + 1]) * half + lane % half
+        jnp.where(lane < span, spans[2 * me], spans[2 * me + 1]) * span + lane % span
     )
     scale = HEAD_WIDTH ** (-0.5)
     exponent = scale * math.log2(math.e)
 
-    def fold(other, first):
-        line = lax.broadcasted_iota(jnp.int32, (2 * rows, 1), 0)
-        base = jnp.full((2 * rows, 1), spans[4 * other], jnp.int32)
-        for i in range(1, 4):
-            base = jnp.where(line >= i * half, spans[4 * other + i], base)
-        k_pos = base * half + line % half
+    def fold(index, count, half, first=False):
+        line = lax.broadcasted_iota(jnp.int32, (count * rows, 1), 0)
+        base = jnp.full((count * rows, 1), spans[2 * index], jnp.int32)
+        for i in range(1, 2 * count):
+            base = jnp.where(line >= i * span, spans[2 * index + i], base)
+        k_pos = base * span + line % span
         bias = jnp.where(k_pos <= q_pos, 0.0, LOW)
-        at = pl.ds(pl.multiple_of(other * 2 * rows, 2 * rows), 2 * rows)
-        for h in range(kv_heads):
+        at = pl.ds(pl.multiple_of(index * rows, rows), count * rows)
+        for h in range(half * pair_heads, (half + 1) * pair_heads):
             band = slice(h * HEAD_WIDTH, (h + 1) * HEAD_WIDTH)
             scores = jnp.dot(k_all[at, band], q_turned[h], preferred_element_type=jnp.float32)
             probs, factors = [], []
@@ -244,45 +257,42 @@
 
     own_k.wait()
     own_v.wait()
-    arrived(0, sibling)
-    arrived(1, sibling)
-    fold(chip, True)
-
-    def gain_two():
-        for copy in p1:
+    for half in range(2):
+        arrived(half, sibling)
+        fold(chip * 2, 2, half, True)
+
+    def gain_chips():
+        for copy in over_dp:
             copy.wait()
-        level[mine_dp] = jnp.sum(part_in[...], axis=0)
+        cross[chip] = jnp.sum(level[...], axis=0)
         copies = []
-        for k in range(1, dp_count):
+        for k in range(1, chips):
             copy = pltpu.make_async_remote_copy(
-                src_ref=level.at[mine_dp],
-                dst_ref=level.at[mine_dp],
-                send_sem=p2_send.at[k],
-                recv_sem=p2_recv.at[k],
-                device_id={"dp": dp_peer(k)},
+                src_ref=cross.at[chip],
+                dst_ref=cross.at[chip],
+                send_sem=p3_send.at[k],
+                recv_sem=p3_recv.at[k],
+                device_id={"ctx": other_chip(k) * 2 + core},
                 device_id_type=MESH,
             )
             copy.start()
             copies.append(copy)
         return copies
 
-    def gain_three(copies):
+    def gain_whole(copies):
         for copy in copies:
             copy.wait()
-        whole[me] = jnp.sum(level[...], axis=0)
-        copies = []
-        for k in range(1, n):
-            copy = pltpu.make_async_remote_copy(
-                src_ref=whole.at[me],
-                dst_ref=whole.at[me],
-                send_sem=p3_send.at[k],
-                recv_sem=p3_recv.at[k],
-                device_id={"ctx": ctx_peer(k)},
-                device_id_type=MESH,
-            )
-            copy.start()
-            copies.append(copy)
-        return copies
+        whole[core] = jnp.sum(cross[...], axis=0)
+        copy = pltpu.make_async_remote_copy(
+            src_ref=whole.at[core],
+            dst_ref=whole.at[core],
+            send_sem=p1_send.at[1],
+            recv_sem=p1_recv.at[1],
+            device_id={"ctx": sibling},
+            device_id_type=MESH,
+        )
+        copy.start()
+        return copy
 
     if square:
         near, far, across = other_chip(1), other_chip(2), other_chip(3)
@@ -293,51 +303,53 @@
         arrived(1, far_c)
         send(1, far_c, near_c, 3)
         send(1, far_c, sibling, 4)
-        p2 = gain_two()
+        over_chips = gain_chips()
+        arrived(0, near * 2 + 1 - core)
+        fold(near * 2, 2, 0)
+        arrived(1, far * 2 + 1 - core)
+        fold(far * 2, 2, 1)
         arrived(1, near_c)
         send(1, near_c, sibling, 5)
         arrived(0, far_c)
         send(0, far_c, sibling, 5)
-        for other in (near, far):
-            arrived(0, other * 2 + 1 - core)
-            arrived(1, other * 2 + 1 - core)
-            fold(other, False)
-        p3 = gain_three(p2)
-        arrived(0, across_c)
-        send(0, across_c, sibling, 6)
-        arrived(1, across_c)
-        send(1, across_c, sibling, 6)
-        arrived(0, across * 2 + 1 - core)
-        arrived(1, across * 2 + 1 - core)
-        fold(across, False)
+        arrived(1, near * 2 + 1 - core)
+        fold(near * 2, 2, 1)
+        arrived(0, far * 2 + 1 - core)
+        fold(far * 2, 2, 0)
+        for half in range(2):
+            arrived(half, across_c)
+            send(half, across_c, sibling, 6)
+        for half in range(2):
+            fold(across_c, 1, half)
+        last = gain_whole(over_chips)
+        for half in range(2):
+            arrived(half, across * 2 + 1 - core)
+            fold(across * 2 + 1 - core, 1, half)
     else:
-        p2 = gain_two()
-        p3 = gain_three(p2)
-
-        def step(k, carry):
+        over_chips = gain_chips()
+
+        def step(k, unused):
             other = (chip + chips - k) % chips
             held = other * 2 + core
-            for which in range(2):
-                arrived(which, held)
-                copy = pltpu.make_async_remote_copy(
-                    src_ref=slot(k_or_v[which], held),
-                    dst_ref=slot(k_or_v[which], held),
-                    send_sem=kv_send.at[which, chips],
-                    recv_sem=kv_recv.at[which, held],
-                    device_id={"ctx": sibling},
-                    device_id_type=MESH,
-                )
-                copy.start()
-                arrived(which, other * 2 + 1 - core)
+            copies = []
+            for half in range(2):
+                arrived(half, held)
+                for which in range(2):
+                    copy = carry(which, half, held, sibling, chips)
+                    copy.start()
+                    copies.append(copy)
+            for half in range(2):
+                arrived(half, other * 2 + 1 - core)
+                fold(other * 2, 2, half)
+            for copy in copies:
                 copy.wait_send()
-            fold(other, False)
-            return carry
+            return unused
 
         lax.fori_loop(1, chips, step, 0)
-
-    for copy in p3:
-        copy.wait()
-    for r in range(n):
+        last = gain_whole(over_chips)
+
+    last.wait()
+    for r in range(2):
         ggrad_buf[:, r * piece : (r + 1) * piece] = whole[r]
     for copy in sends:
         copy.wait_send()
@@ -381,7 +393,7 @@
     width = resid.shape[2]
     heads, kv_heads = q_width // HEAD_WIDTH, kv_width // HEAD_WIDTH
     group = heads // kv_heads
-    piece = width // n
+    piece = width // 2
     f32, bf16 = jnp.float32, jnp.bfloat16
     dma = pltpu.SemaphoreType.DMA
     lanes = max(8, n // 2 + 1)
@@ -408,19 +420,20 @@
             pltpu.VMEM((rows, width), bf16),
             pltpu.VMEM((1, width), f32),
             pltpu.VMEM((8, width), f32),
-            pltpu.VMEM((n, 1, piece), f32),
-            pltpu.VMEM((n, 1, piece), f32),
+            pltpu.VMEM((2, 1, piece), f32),
+            pltpu.VMEM((1, 1, piece), f32),
             pltpu.VMEM((dp_count, 1, piece), f32),
-            pltpu.VMEM((n, 1, piece), f32),
+            pltpu.VMEM((n // 2, 1, piece), f32),
+            pltpu.VMEM((2, 1, piece), f32),
             dma((7,)),
-            dma((2, lanes)),
-            dma((2, n)),
-            dma((n,)),
-            dma((n,)),
+            dma((2, 2, lanes)),
+            dma((2, 2, n)),
+            dma((2,)),
+            dma((2,)),
             dma((dp_count,)),
             dma((dp_count,)),
-            dma((n,)),
-            dma((n,)),
+            dma((n // 2,)),
+            dma((n // 2,)),
         ],
         compiler_params=pltpu.CompilerParams(collective_id=0, has_side_effects=True),
     )(

time: 24.8 us -> 22.1 us (0.89)
  Pallas kernels: 24 us -> 21.3 us
    pallas_call x1, Pallas kernels: 22.8 us -> 20.1 us  [per_device(): pl.pallas_call(functools.partial(kernel, n, dp_count, heads, kv_heads), o...]
where the time goes in v3:
time: 22.1 us; the launch traced here: 21.9 us
  Pallas kernels  21.3 us (96%)
  between operations  0.64 us (3%)
    pallas_call x1, Pallas kernels, per_device(): pl.pallas_call(functools.partial(kernel, n, dp_count, heads, kv_heads), o...  20.1 us
    pallas_call x1, Pallas kernels, per_device(): pl.pallas_call(functools.partial(finish, heads, kv_heads), out_shape=(jax...  1.2 us

profile of v3, /device:TPU:0, one launch (start us, length us, event | category | flops | bytes accessed | tf_op | source)
XLA Modules:
  0.0 21.9 jit_solution(18089055085118967630)
XLA Ops:
  0.6 20.1 %shard_map.102 = (f32[4,128,512]{2,1,0:T(8,128)S(1)}, f32[4,512]{1,0:T(4,128)S(1)}, f32[4,512]{1,0:T(4,128)S(1)}, bf16[128,4096]{1,0:T(8,128)(2,1)S(1)}, f32[1,4096]{1,0:T(1,128)S(1)}) custom-call(bf16[128,2048]{1,0:T(8,128)(2,1)} %bitcast.12, bf16[128,512]{1,0:T(8,128)(2,1)} %bitcast.13, bf16[128,512]{1,0:T(8,128)(2,1)} %bitcast.14, s32[16]{0:T(128)} %span_hbm.1, ...), custom_call_target="tpu_custom_call" | custom-call | tf_op jit(solution)/shard_map/pallas_call | solution.py:408
  20.7 1.2 %shard_map.103 = (bf16[128,2048]{1,0:T(8,128)(2,1)}, f32[16,128]{1,0:T(8,128)}, bf16[128,4096]{1,0:T(8,128)(2,1)}, f32[1,4096]{1,0:T(1,128)}) custom-call(f32[4,128,512]{2,1,0:T(8,128)S(1)} %get-tuple-element.13.summed, f32[4,512]{1,0:T(4,128)S(1)} %get-tuple-element.14.tops, f32[4,512]{1,0:T(4,128)S(1)} %get-tuple-element.15.totals, ...), custom_call_target="tpu_custom_call" | custom-call | tf_op jit(solution)/shard_map/pallas_call | solution.py:448

commit v4 on v3

--- a/solution.py
+++ b/solution.py
@@ -112,7 +112,7 @@
     def carry(which, half, index, target, lane, first=False):
         held = part_of(k_or_v[which], half, index)
         return pltpu.make_async_remote_copy(
-            src_ref=source[which].at[:, half * cut : (half + 1) * cut] if first else held,
+            src_ref=held,
             dst_ref=held,
             send_sem=kv_send.at[which, half, lane],
             recv_sem=kv_recv.at[which, half, index],
@@ -130,6 +130,8 @@
         for which in range(2):
             carry(which, half, index, sibling, 0).wait_recv()
 
+    own_k.wait()
+    own_v.wait()
     pl.semaphore_wait(barrier, chips + dp_count - 1)
 
     if square:
@@ -224,9 +226,17 @@
         k_pos = base * span + line % span
         bias = jnp.where(k_pos <= q_pos, 0.0, LOW)
         at = pl.ds(pl.multiple_of(index * rows, rows), count * rows)
+        products = [
+            jnp.dot(
+                k_all[at, h * HEAD_WIDTH : (h + 1) * HEAD_WIDTH],
+                q_turned[h],
+                preferred_element_type=jnp.float32,
+            )
+            for h in range(half * pair_heads, (half + 1) * pair_heads)
+        ]
         for h in range(half * pair_heads, (half + 1) * pair_heads):
             band = slice(h * HEAD_WIDTH, (h + 1) * HEAD_WIDTH)
-            scores = jnp.dot(k_all[at, band], q_turned[h], preferred_element_type=jnp.float32)
+            scores = products[h - half * pair_heads]
             probs, factors = [], []
             for g in range(group):
                 lanes = slice(g * rows, (g + 1) * rows)
@@ -255,8 +265,6 @@
             else:
                 summed[h] = summed[h] * jnp.concatenate(factors, axis=1) + added
 
-    own_k.wait()
-    own_v.wait()
     for half in range(2):
         arrived(half, sibling)
         fold(chip * 2, 2, half, True)
@@ -312,10 +320,12 @@
         send(1, near_c, sibling, 5)
         arrived(0, far_c)
         send(0, far_c, sibling, 5)
+        fold(near_c, 1, 1)
+        fold(far_c, 1, 0)
         arrived(1, near * 2 + 1 - core)
-        fold(near * 2, 2, 1)
+        fold(near * 2 + 1 - core, 1, 1)
         arrived(0, far * 2 + 1 - core)
-        fold(far * 2, 2, 0)
+        fold(far * 2 + 1 - core, 1, 0)
         for half in range(2):
             arrived(half, across_c)
             send(half, across_c, sibling, 6)

time: 22.1 us -> 20.7 us (0.937)
  Pallas kernels: 21.3 us -> 19.9 us
    pallas_call x1, Pallas kernels: 20.1 us -> 18.7 us  [per_device(): pl.pallas_call(functools.partial(kernel, n, dp_count, heads, kv_heads), o...]
where the time goes in v4:
time: 20.7 us; the launch traced here: 20.5 us
  Pallas kernels  19.9 us (96%)
  between operations  0.64 us (3%)
    pallas_call x1, Pallas kernels, per_device(): pl.pallas_call(functools.partial(kernel, n, dp_count, heads, kv_heads), o...  18.7 us
    pallas_call x1, Pallas kernels, per_device(): pl.pallas_call(functools.partial(finish, heads, kv_heads), out_shape=(jax...  1.2 us

profile of v4, /device:TPU:0, one launch (start us, length us, event | category | flops | bytes accessed | tf_op | source)
XLA Modules:
  0.0 20.5 jit_solution(17485203320934077361)
XLA Ops:
  0.6 18.7 %shard_map.102 = (f32[4,128,512]{2,1,0:T(8,128)S(1)}, f32[4,512]{1,0:T(4,128)S(1)}, f32[4,512]{1,0:T(4,128)S(1)}, bf16[128,4096]{1,0:T(8,128)(2,1)S(1)}, f32[1,4096]{1,0:T(1,128)S(1)}) custom-call(bf16[128,2048]{1,0:T(8,128)(2,1)} %bitcast.12, bf16[128,512]{1,0:T(8,128)(2,1)} %bitcast.13, bf16[128,512]{1,0:T(8,128)(2,1)} %bitcast.14, s32[16]{0:T(128)} %span_hbm.1, ...), custom_call_target="tpu_custom_call" | custom-call | tf_op jit(solution)/shard_map/pallas_call | solution.py:418
  19.3 1.2 %shard_map.103 = (bf16[128,2048]{1,0:T(8,128)(2,1)}, f32[16,128]{1,0:T(8,128)}, bf16[128,4096]{1,0:T(8,128)(2,1)}, f32[1,4096]{1,0:T(1,128)}) custom-call(f32[4,128,512]{2,1,0:T(8,128)S(1)} %get-tuple-element.13.summed, f32[4,512]{1,0:T(4,128)S(1)} %get-tuple-element.14.tops, f32[4,512]{1,0:T(4,128)S(1)} %get-tuple-element.15.totals, ...), custom_call_target="tpu_custom_call" | custom-call | tf_op jit(solution)/shard_map/pallas_call | solution.py:458
